TPU v7x, 512 devices: a 4x2x32 block of a 4x8x32 slice. The times are simulated.
512 devices in a mesh: rep: 2 (over y), tp: 32 (over z), ep: 8 (over x, core).
Axes of the slice: x: 4, y: 2, z: 32, core: 2. Of those that a mesh axis runs over, the one named last changes fastest.
The devices are a block of a 4x8x32 slice.
Arguments:
- tokens: bfloat16 [1536, 3072], P(('rep', 'ep'), 'tp'), parts along dimension 0, may hold values from -6 to 6
- routing: int32 [1536, 2], P(('rep', 'ep')), parts along dimension 0, may hold values from 0 to 7, all different within a row; in each aligned block of 96 rows (0 to 95, 96 to 191, ...) at most 30 rows name the same one
- route_gates: float32 [1536, 2], P(('rep', 'ep')), parts along dimension 0, may hold values from 0.2 to 1
- expert_gate: bfloat16 [8, 3072, 8192], P('ep', None, 'tp'), may hold values from -0.109375 to 0.109375
- expert_up: bfloat16 [8, 3072, 8192], P('ep', None, 'tp'), may hold values from -0.109375 to 0.109375
- expert_down: bfloat16 [8, 8192, 3072], P('ep', 'tp'), may hold values from -0.0625 to 0.0625
Outputs:
- mixture: bfloat16 [1536, 3072], P(('rep', 'ep'), 'tp'), parts along dimension 0
There are 2 independent parts, one for each index of `rep`. A program takes and returns all parts, laid end to end along the dimension named above; an argument that names none is the same for every part. Nothing has to cross between parts.
Inputs may be any that keep to these rules, and one draw needn't show every extreme that they name: `routing`: each token names two different experts. In each aligned block of 96 tokens (the rows of one index of ep) no expert is named by more than 30 tokens, a bound that some block reaches.
All inputs are finite; a program needn't handle non-finite values.
Results may differ from a plain program's by a relative error of at most 0.0085.
Values may be sent and summed in bfloat16 or wider, within the bound.
No kernel may reach another device: no remote copies, remote signals or barrier semaphores. Data moves between devices by JAX's collectives and lax.ppermute only.
A program may use at most 64 MiB of HBM per device.

v0:
```python
import jax
import jax.numpy as jnp
from jax import lax
from jax.sharding import Mesh
from jax.sharding import PartitionSpec as P

REP_EP = ("rep", "ep")
TP = ("hi", "lo")
BF = jnp.bfloat16
F32 = jnp.float32
LO = 2


def slot_tables(routing, route_gates, experts, rows):
    tok_count, choices_n = routing.shape
    flat_ids = routing.reshape(-1)
    onehot = (flat_ids[:, None] == jnp.arange(experts, dtype=jnp.int32)[None, :]).astype(BF)
    n = tok_count * choices_n
    earlier = (jnp.arange(n)[None, :] < jnp.arange(n)[:, None]).astype(BF)
    before = jnp.dot(earlier, onehot, preferred_element_type=F32)
    position = jnp.sum(before * onehot.astype(F32), axis=1).astype(jnp.int32)
    slot = (flat_ids * rows + position).reshape(tok_count, choices_n)
    picked = slot[:, :, None] == jnp.arange(experts * rows, dtype=jnp.int32)[None, None, :]
    dispatch = picked.astype(F32).sum(axis=1).astype(BF)
    combine = jnp.where(picked, route_gates[:, :, None], 0.0).sum(axis=1)
    return (dispatch, combine)


def body(tokens, routing, route_gates, expert_gate, expert_up, expert_down):
    ep_count = lax.axis_size("ep")
    hi_count = lax.axis_size("hi")
    tok_count, feat = tokens.shape
    capacity = 2 * tok_count // ep_count + tok_count // 16
    rows = -(-capacity // 8) * 8
    slots = ep_count * rows
    wide = hi_count * feat
    hidden_n = expert_gate.shape[2]
    gathered = lax.all_gather(tokens.T, "hi", axis=0, tiled=True)
    dispatch, combine = slot_tables(routing, route_gates, ep_count, rows)
    packed = lax.dot_general(
        dispatch, gathered, (((0,), (1,)), ((), ())), preferred_element_type=F32
    ).astype(BF)
    sent = jnp.broadcast_to(packed.reshape(1, ep_count, rows, wide), (LO, ep_count, rows, wide))
    got = lax.all_to_all(
        sent.reshape(LO * ep_count, rows, wide), ("lo", "ep"), 0, 0, tiled=True
    ).reshape(LO, slots, wide)

    def by_lo(w):
        return (
            w.reshape(hi_count, LO, feat, hidden_n)
            .transpose(1, 0, 2, 3)
            .reshape(LO, wide, hidden_n)
        )

    w_gate, w_up = (by_lo(expert_gate), by_lo(expert_up))
    gate = sum((jnp.dot(got[i], w_gate[i], preferred_element_type=F32) for i in range(LO)))
    up = sum((jnp.dot(got[i], w_up[i], preferred_element_type=F32) for i in range(LO)))
    hidden = (jax.nn.silu(gate) * up).astype(BF)
    w_down = (
        expert_down.reshape(hidden_n, hi_count, LO, feat)
        .transpose(2, 0, 1, 3)
        .reshape(LO, hidden_n, wide)
    )
    part = jnp.stack(
        [jnp.dot(hidden, w_down[i], preferred_element_type=F32).astype(BF) for i in range(LO)]
    )
    back = lax.all_to_all(
        part.reshape(LO * ep_count, rows, wide), ("lo", "ep"), 0, 0, tiled=True
    ).reshape(LO * slots, wide)
    weights = jnp.concatenate([combine] * LO, axis=1).astype(BF)
    mixed = lax.dot_general(
        back, weights, (((0,), (1,)), ((), ())), preferred_element_type=F32
    ).astype(BF)
    shares = lax.all_to_all(mixed.reshape(hi_count, feat, tok_count), "hi", 0, 0, tiled=True)
    return jnp.sum(shares.astype(F32), axis=0).astype(BF).T


def solution(mesh):
    finer = Mesh(
        mesh.devices.reshape(mesh.shape["rep"], mesh.shape["tp"] // LO, LO, mesh.shape["ep"]),
        ("rep", "hi", "lo", "ep"),
    )
    placed = (
        P(REP_EP, TP),
        P(REP_EP, None),
        P(REP_EP, None),
        P("ep", None, TP),
        P("ep", None, TP),
        P("ep", TP, None),
    )
    return jax.shard_map(
        body, mesh=finer, in_specs=placed, out_specs=P(REP_EP, TP), check_vma=False
    )
```

profile of v0, /device:TPU:166, one launch (start us, length us, event | category | flops | bytes accessed | tf_op | source)
XLA Modules:
  0.0 195.5 jit_solution(637232276068174422)
XLA Ops:
  0.0 0.8 copy.28
  0.8 0.1 eq.28
  0.9 0.2 fusion.4
  1.1 0.1 convert_element_type.42
  1.3 0.7 multiply_add_fusion
  2.0 0.8 copy.30
  2.9 68.8 %all_gather.3 = bf16[1536,96]{1,0:T(8,128)(2,1)S(1)} all-gather(bf16[96,96]{1,0:T(8,128)(2,1)S(1)} %bitcast.60), channel_id=1, replica_groups=mesh['rep'=2,'hi'=16,'lo'=2,'ep'=8] {'hi'}, dimensions={0}, use_global_device_ids=true | all-gather | bytes 313344 | tf_op jit(solution)/shard_map/all_gather | solution.py:38
  71.7 0.8 select_reduce_fusion
  72.5 0.4 convolution_convert_fusion.2
  72.9 1.3 broadcast_in_dim.25
  74.2 6.2 %all-to-all-start = ((bf16[16,32,1536]{2,1,0:T(8,128)(2,1)}), bf16[16,32,1536]{2,1,0:T(8,128)(2,1)S(1)}, u32[]{:S(2)}, u32[]{:S(2)}) async-start(bf16[16,32,1536]{2,1,0:T(8,128)(2,1)} %bitcast.2), calls=%async_computation | async-start | bytes 3145728 | tf_op jit(solution)/shard_map/all_to_all | solution.py:44
  80.4 1.7 copy.31
  82.1 2.7 %fusion.13 = (bf16[1,16,96,256]{3,2,0,1:T(8,128)(2,1)}, bf16[1,16,96,256]{3,2,0,1:T(8,128)(2,1)}) fusion(bf16[2,16,96,256]{3,2,0,1:T(8,128)(2,1)} %bitcast.57), kind=kLoop, calls=%fused_computation.27 | loop fusion | bytes 3145728 | tf_op jit(solution)/shard_map/slice | solution.py:56
  84.9 1.3 fusion.14
  86.2 1.3 fusion.12
  87.5 14.4 %all-to-all-done = bf16[16,32,1536]{2,1,0:T(8,128)(2,1)S(1)} async-done(((bf16[16,32,1536]{2,1,0:T(8,128)(2,1)}), bf16[16,32,1536]{2,1,0:T(8,128)(2,1)S(1)}, u32[]{:S(2)}, u32[]{:S(2)}) %all-to-all-start) | async-done | bytes 1572896 | tf_op jit(solution)/shard_map/all_to_all | solution.py:44
  102.0 0.4 fusion.16
  102.4 0.7 copy-done.1
  103.1 0.4 fusion.17
  103.5 0.4 convolution_add_fusion.1
  103.9 0.4 copy-done.6
  104.3 0.4 fusion.3
  104.7 0.4 copy-done.3
  105.0 0.4 fusion
  105.4 0.4 copy-done.2
  105.8 0.4 fusion.1
  106.3 0.1 pad_maximum_fusion
  106.4 24.2 %all_to_all.15 = bf16[16,32,1536]{2,1,0:T(8,128)(2,1)S(1)} all-to-all(bf16[16,32,1536]{2,1,0:T(8,128)(2,1)S(1)} %bitcast.47), channel_id=1, replica_groups=mesh['rep'=2,'hi'=16,'lo'=2,'ep'=8] {'lo','ep'}, dimensions={0} | all-to-all | bytes 3145728 | tf_op jit(solution)/shard_map/all_to_all | solution.py:67
  130.7 0.4 convolution_convert_fusion.3
  131.0 0.3 reshape.60
  131.5 63.3 %all_to_all.16 = bf16[16,96,96]{1,2,0:T(8,128)(2,1)S(1)} all-to-all(bf16[16,96,96]{1,2,0:T(8,128)(2,1)S(1)} %copy.32), channel_id=1, replica_groups=mesh['rep'=2,'hi'=16,'lo'=2,'ep'=8] {'hi'}, dimensions={0} | all-to-all | bytes 589824 | tf_op jit(solution)/shard_map/all_to_all | solution.py:74
  194.8 0.7 reduce_sum.42
  (14 shorter events, 0.3 us)
Async XLA Ops:
  74.2 27.6 %all-to-all-start = ((bf16[16,32,1536]{2,1,0:T(8,128)(2,1)}), bf16[16,32,1536]{2,1,0:T(8,128)(2,1)S(1)}, u32[]{:S(2)}, u32[]{:S(2)}) async-start(bf16[16,32,1536]{2,1,0:T(8,128)(2,1)} %bitcast.2), calls=%async_computation | async-start | bytes 3145728 | tf_op jit(solution)/shard_map/all_to_all | solution.py:44
  82.1 2.8 %copy-start.5 = (bf16[1,3072,256]{2,1,0:T(8,128)(2,1)S(1)}, bf16[1,3072,256]{2,1,0:T(8,128)(2,1)}, u32[]{:S(2)}) copy-start(bf16[1,3072,256]{2,1,0:T(8,128)(2,1)} %param.10) | copy-start | bytes 4718596
  87.5 14.5 %copy-start = (bf16[1,16,96,256]{3,2,0,1:T(8,128)(2,1)S(1)}, bf16[1,16,96,256]{3,2,0,1:T(8,128)(2,1)}, u32[]{:S(2)}) copy-start(bf16[1,16,96,256]{3,2,0,1:T(8,128)(2,1)} %get-tuple-element.10) | copy-start | bytes 2359300
  101.9 1.1 copy-start.1
  102.0 1.5 copy-start.4
  103.1 1.2 copy-start.6
  103.8 1.2 copy-start.3
  104.7 1.2 copy-start.2
where the time goes:
time: 196 us; the launch traced here: 195 us
  blocking collectives  156 us (80%)
  waiting for transfers between devices  14.4 us (7%)
  local copies, waits for them, and re-layouts  12.8 us (7%)
  starting transfers between devices  6.17 us (3%)
  matrix products  3.21 us (2%)
  other arithmetic  2.36 us (1%)
    all_gather x1, blocking collectives, body(): gathered = lax.all_gather(tokens.T, 'hi', axis=0, tiled=True)  68.8 us
    all_to_all x1, blocking collectives, body(): lax.all_to_all(mixed.reshape(hi_count, feat, tok_count), 'hi', 0, 0, tile...  63.3 us
    all_to_all x1, blocking collectives, body(): lax.all_to_all(part.reshape(LO * ep_count, rows, wide), ('lo', 'ep'), 0,...  24.2 us
    all_to_all x1, waiting for transfers between devices, body(): lax.all_to_all(sent.reshape(LO * ep_count, rows, wide), ('lo', 'ep'), 0,...  14.4 us
    all_to_all x1, starting transfers between devices, body(): lax.all_to_all(sent.reshape(LO * ep_count, rows, wide), ('lo', 'ep'), 0,...  6.17 us
    unnamed x17, local copies, waits for them, and re-layouts  5.25 us
  transfers between devices with their start and end apart: 1, of which 1 were waited for; matrix products, arithmetic and copies ran while one was open for 4% of the time, Pallas kernels for 0%

commit v1 on v0

--- a/solution.py
+++ b/solution.py
@@ -35,7 +35,9 @@
     slots = ep_count * rows
     wide = hi_count * feat
     hidden_n = expert_gate.shape[2]
-    gathered = lax.all_gather(tokens.T, "hi", axis=0, tiled=True)
+    gathered = jnp.concatenate(
+        lax.all_to_all(jnp.stack([tokens.T] * lax.axis_size("hi")), "hi", 0, 0), axis=0
+    )
     dispatch, combine = slot_tables(routing, route_gates, ep_count, rows)
     packed = lax.dot_general(
         dispatch, gathered, (((0,), (1,)), ((), ())), preferred_element_type=F32

time: 196 us -> 210 us (1.071)
  blocking collectives: 156 us -> 81.9 us
  starting transfers between devices: 6.17 us -> 60.4 us
  waiting for transfers between devices: 14.4 us -> 47.3 us
    all_gather x1 -> x0, blocking collectives: 68.8 us -> none  [body(): gathered = lax.all_gather(tokens.T, 'hi', axis=0, tiled=True)]
    all_to_all x0 -> x1, starting transfers between devices: none -> 42.2 us  [body(): lax.all_to_all(jnp.stack([tokens.T] * lax.axis_size('hi')), 'hi', 0, 0)]
    all_to_all x0 -> x1, waiting for transfers between devices: none -> 33 us  [body(): lax.all_to_all(jnp.stack([tokens.T] * lax.axis_size('hi')), 'hi', 0, 0)]
    all_to_all x1, starting transfers between devices: 6.17 us -> 18.2 us  [body(): lax.all_to_all(sent.reshape(LO * ep_count, rows, wide), ('lo', 'ep'), 0,...]
    all_to_all x1, blocking collectives: 63.3 us -> 57.6 us  [body(): lax.all_to_all(mixed.reshape(hi_count, feat, tok_count), 'hi', 0, 0, tile...]
    unnamed x17 -> x16, local copies, waits for them, and re-layouts: 5.25 us -> 4.42 us
  transfers between devices with their start and end apart: 1 -> 2, of which waited for: 1 -> 2; matrix products, arithmetic and copies ran while one was open for 4% -> 5% of each run, Pallas kernels for 0% -> 0%
where the time goes in v1:
time: 210 us; the launch traced here: 209 us
  blocking collectives  81.9 us (39%)
  starting transfers between devices  60.4 us (29%)
  waiting for transfers between devices  47.3 us (23%)
  local copies, waits for them, and re-layouts  13.6 us (6%)
  matrix products  3.21 us (2%)
  other arithmetic  2.36 us (1%)
    all_to_all x1, blocking collectives, body(): lax.all_to_all(mixed.reshape(hi_count, feat, tok_count), 'hi', 0, 0, tile...  57.6 us
    all_to_all x1, starting transfers between devices, body(): lax.all_to_all(jnp.stack([tokens.T] * lax.axis_size('hi')), 'hi', 0, 0)  42.2 us
    all_to_all x1, waiting for transfers between devices, body(): lax.all_to_all(jnp.stack([tokens.T] * lax.axis_size('hi')), 'hi', 0, 0)  33 us
    all_to_all x1, blocking collectives, body(): lax.all_to_all(part.reshape(LO * ep_count, rows, wide), ('lo', 'ep'), 0,...  24.2 us
    all_to_all x1, starting transfers between devices, body(): lax.all_to_all(sent.reshape(LO * ep_count, rows, wide), ('lo', 'ep'), 0,...  18.2 us
    all_to_all x1, waiting for transfers between devices, body(): lax.all_to_all(sent.reshape(LO * ep_count, rows, wide), ('lo', 'ep'), 0,...  14.4 us
    unnamed x16, local copies, waits for them, and re-layouts  4.42 us
  transfers between devices with their start and end apart: 2, of which 2 were waited for; matrix products, arithmetic and copies ran while one was open for 5% of the time, Pallas kernels for 0%

profile of v1, /device:TPU:166, one launch (start us, length us, event | category | flops | bytes accessed | tf_op | source)
XLA Modules:
  0.0 209.0 jit_solution(2862732457851859951)
XLA Ops:
  0.0 0.8 copy.32
  0.8 0.8 stack.8
  1.6 42.2 %all-to-all-start = ((bf16[16,96,96]{2,1,0:T(8,128)(2,1)}), bf16[16,96,96]{2,1,0:T(8,128)(2,1)S(1)}, u32[]{:S(2)}, u32[]{:S(2)}) async-start(bf16[16,96,96]{2,1,0:T(8,128)(2,1)} %stack.8), calls=%async_computation | async-start | bytes 786432 | tf_op jit(solution)/shard_map/all_to_all | solution.py:39
  43.9 0.8 copy.30
  44.8 0.2 fusion.4
  45.2 0.7 multiply_add_fusion
  45.9 0.8 select_reduce_fusion
  46.7 33.0 %all-to-all-done = bf16[16,96,96]{2,1,0:T(8,128)(2,1)S(1)} async-done(((bf16[16,96,96]{2,1,0:T(8,128)(2,1)}), bf16[16,96,96]{2,1,0:T(8,128)(2,1)S(1)}, u32[]{:S(2)}, u32[]{:S(2)}) %all-to-all-start) | async-done | bytes 294944 | tf_op jit(solution)/shard_map/all_to_all | solution.py:39
  79.7 0.4 convolution_convert_fusion.2
  80.1 1.3 broadcast_in_dim.25
  81.4 18.2 %all-to-all-start.1 = ((bf16[16,32,1536]{2,1,0:T(8,128)(2,1)}), bf16[16,32,1536]{2,1,0:T(8,128)(2,1)S(1)}, u32[]{:S(2)}, u32[]{:S(2)}) async-start(bf16[16,32,1536]{2,1,0:T(8,128)(2,1)} %bitcast.3), calls=%async_computation.1 | async-start | bytes 3145728 | tf_op jit(solution)/shard_map/all_to_all | solution.py:46
  99.6 1.7 copy.33
  101.3 2.7 %fusion.13 = (bf16[1,16,96,256]{3,2,0,1:T(8,128)(2,1)}, bf16[1,16,96,256]{3,2,0,1:T(8,128)(2,1)}) fusion(bf16[2,16,96,256]{3,2,0,1:T(8,128)(2,1)} %bitcast.58), kind=kLoop, calls=%fused_computation.27 | loop fusion | bytes 3145728 | tf_op jit(solution)/shard_map/slice | solution.py:58
  104.1 1.3 fusion.14
  105.4 1.3 fusion.12
  106.7 14.4 %all-to-all-done.1 = bf16[16,32,1536]{2,1,0:T(8,128)(2,1)S(1)} async-done(((bf16[16,32,1536]{2,1,0:T(8,128)(2,1)}), bf16[16,32,1536]{2,1,0:T(8,128)(2,1)S(1)}, u32[]{:S(2)}, u32[]{:S(2)}) %all-to-all-start.1) | async-done | bytes 1572896 | tf_op jit(solution)/shard_map/all_to_all | solution.py:46
  121.2 0.4 fusion.16
  121.5 0.7 copy-done.1
  122.3 0.4 fusion.17
  122.7 0.4 convolution_add_fusion.1
  123.1 0.4 copy-done.6
  123.5 0.4 fusion.3
  123.9 0.4 copy-done.3
  124.2 0.4 fusion
  124.6 0.4 copy-done.2
  125.0 0.4 fusion.1
  125.4 0.1 pad_maximum_fusion
  125.6 24.2 %all_to_all.20 = bf16[16,32,1536]{2,1,0:T(8,128)(2,1)S(1)} all-to-all(bf16[16,32,1536]{2,1,0:T(8,128)(2,1)S(1)} %bitcast.48), channel_id=1, replica_groups=mesh['rep'=2,'hi'=16,'lo'=2,'ep'=8] {'lo','ep'}, dimensions={0} | all-to-all | bytes 3145728 | tf_op jit(solution)/shard_map/all_to_all | solution.py:69
  149.9 0.4 convolution_convert_fusion.3
  150.2 0.3 reshape.66
  150.7 57.6 %all_to_all.21 = bf16[16,96,96]{1,2,0:T(8,128)(2,1)S(1)} all-to-all(bf16[16,96,96]{1,2,0:T(8,128)(2,1)S(1)} %copy.34), channel_id=1, replica_groups=mesh['rep'=2,'hi'=16,'lo'=2,'ep'=8] {'hi'}, dimensions={0} | all-to-all | bytes 589824 | tf_op jit(solution)/shard_map/all_to_all | solution.py:76
  208.3 0.7 reduce_sum.42
  (16 shorter events, 0.6 us)
Async XLA Ops:
  1.6 78.0 %all-to-all-start = ((bf16[16,96,96]{2,1,0:T(8,128)(2,1)}), bf16[16,96,96]{2,1,0:T(8,128)(2,1)S(1)}, u32[]{:S(2)}, u32[]{:S(2)}) async-start(bf16[16,96,96]{2,1,0:T(8,128)(2,1)} %stack.8), calls=%async_computation | async-start | bytes 786432 | tf_op jit(solution)/shard_map/all_to_all | solution.py:39
  81.4 39.7 %all-to-all-start.1 = ((bf16[16,32,1536]{2,1,0:T(8,128)(2,1)}), bf16[16,32,1536]{2,1,0:T(8,128)(2,1)S(1)}, u32[]{:S(2)}, u32[]{:S(2)}) async-start(bf16[16,32,1536]{2,1,0:T(8,128)(2,1)} %bitcast.3), calls=%async_computation.1 | async-start | bytes 3145728 | tf_op jit(solution)/shard_map/all_to_all | solution.py:46
  101.3 2.8 %copy-start.5 = (bf16[1,3072,256]{2,1,0:T(8,128)(2,1)S(1)}, bf16[1,3072,256]{2,1,0:T(8,128)(2,1)}, u32[]{:S(2)}) copy-start(bf16[1,3072,256]{2,1,0:T(8,128)(2,1)} %param.10) | copy-start | bytes 4718596
  106.6 14.5 %copy-start = (bf16[1,16,96,256]{3,2,0,1:T(8,128)(2,1)S(1)}, bf16[1,16,96,256]{3,2,0,1:T(8,128)(2,1)}, u32[]{:S(2)}) copy-start(bf16[1,16,96,256]{3,2,0,1:T(8,128)(2,1)} %get-tuple-element.10) | copy-start | bytes 2359300
  121.1 1.1 copy-start.1
  121.2 1.5 copy-start.4
  122.3 1.2 copy-start.6
  123.0 1.2 copy-start.3
  123.8 1.2 copy-start.2
